TPU v7x, 8 devices: a whole 2x2x1 slice. The times are simulated.
8 devices in a mesh: dp: 1 (over z), tp: 2 (over y), sp: 4 (over x, core).
Axes of the slice: x: 2, y: 2, z: 1, core: 2. Of those that a mesh axis runs over, the one named last changes fastest.
Arguments:
- hidden: bfloat16 [256, 7168], P('dp')
- lat_cache: bfloat16 [256, 2048, 512], P('dp', 'sp')
- rope_cache: bfloat16 [256, 2048, 64], P('dp', 'sp')
- positions: int32 [256], P('dp')
- w_dq: bfloat16 [7168, 1536], replicated
- gain_q: bfloat16 [1536], replicated
- w_dkv: bfloat16 [7168, 576], replicated
- gain_kv: bfloat16 [512], replicated
- w_uq: bfloat16 [1536, 128, 192], P(None, 'tp')
- w_uk: bfloat16 [512, 128, 128], P(None, 'tp')
- w_uv: bfloat16 [512, 128, 128], P(None, 'tp')
- w_out: bfloat16 [16384, 7168], P('tp')
Outputs:
- output 1: bfloat16 [256, 7168], P('dp')
- output 2: bfloat16 [256, 2048, 512], P('dp', 'sp')
- output 3: bfloat16 [256, 2048, 64], P('dp', 'sp')
All inputs are finite; a program needn't handle non-finite values.
Results may differ from a plain program's by a relative error of at most 0.0116136.
Values sent between devices are 32-bit elements.
A program may use at most 2 GiB of HBM per device.

v0:
```python
import functools
import math
import jax
import jax.numpy as jnp
from jax import lax
from jax.experimental import pallas as pl
from jax.experimental.pallas import tpu as pltpu
from jax.sharding import PartitionSpec as P

EPSILON = 1e-6
ROPE_BASE = 50000.0
YARN_MSCALE = 1.0 + 0.1 * math.log(32.0)
MASK_VALUE = -1e30
MESH = pl.DeviceIdType.MESH
GROUP = 8
SETS = 4
AHEAD = 2
UNROLL = 4
VMEM_LIMIT = 66 * 1000 * 1000
SIZES = (96, 112, 256)


def rms_norm(values, gain):
    vals32 = values.astype(jnp.float32)
    inv_rms = lax.rsqrt(jnp.mean(vals32 * vals32, axis=-1, keepdims=True) + EPSILON)
    return vals32 * inv_rms * gain.astype(jnp.float32)


def rope_tables(positions, rope_dim):
    half_dim = rope_dim // 2
    inv_freq = ROPE_BASE ** (-jnp.arange(half_dim).astype(jnp.float32) / half_dim)
    angles = positions.astype(jnp.float32)[:, None] * inv_freq[None, :]
    return jnp.cos(angles), jnp.sin(angles)


def rotate_pairs(values, cos_t, sin_t):
    half_dim = values.shape[-1] // 2
    first_half = values[..., :half_dim]
    second_half = values[..., half_dim:]
    return jnp.concatenate([first_half * cos_t - second_half * sin_t, second_half * cos_t + first_half * sin_t], axis=-1)


def query_kernel(cq, cos_t, sin_t, wq, wk, q_out, q_buf, k_buf, a_buf, r_buf):
    rows = cq.shape[0]
    heads, width, depth = wq.shape
    rank = wk.shape[0]
    nope = wk.shape[2]
    half = (width - nope) // 2
    nt = (((1,), (1,)), ((), ()))
    k_buf[...] = wk[...].astype(jnp.float32).reshape(rank * heads, nope)
    q_buf[...] = lax.dot_general(wq[...].reshape(heads * width, depth), cq[...], nt, preferred_element_type=jnp.float32)
    for h in range(heads):
        q = q_buf[h * width:(h + 1) * width, :].astype(jnp.bfloat16)
        r1 = q[nope:nope + half].astype(jnp.float32)
        r2 = q[nope + half:].astype(jnp.float32)
        r = jnp.concatenate([r1 * cos_t[...] - r2 * sin_t[...], r2 * cos_t[...] + r1 * sin_t[...],
                             jnp.zeros((128 - 2 * half, rows), jnp.float32)], axis=0)
        r_buf[pl.ds(h, rows, stride=heads), :] = r.T
        wk_h = k_buf[pl.ds(h, rank, stride=heads), :].astype(jnp.bfloat16)
        qa = lax.dot_general(q[:nope].T, wk_h, nt, preferred_element_type=jnp.float32)
        for c in range(rank // 128):
            a_buf[c, pl.ds(h, rows, stride=heads), :] = qa[:, c * 128:(c + 1) * 128]
    for c in range(rank // 128):
        q_out[:, :, c * 128:(c + 1) * 128] = a_buf[c].reshape(rows, heads, 128).astype(q_out.dtype)
    q_out[:, :, rank:] = r_buf[...].reshape(rows, heads, 128).astype(q_out.dtype)


def queries(cq, cos_w, sin_w, w_uq, w_uk):
    rows, qrank = cq.shape
    wq = w_uq.transpose(1, 2, 0)
    heads, width, _ = wq.shape
    rank, _, nope = w_uk.shape
    hb = 8
    rope_dim = width - nope
    return pl.pallas_call(
        query_kernel,
        grid=(heads // hb,),
        in_specs=[
            pl.BlockSpec((rows, qrank), lambda i: (0, 0)),
            pl.BlockSpec((rope_dim // 2, rows), lambda i: (0, 0)),
            pl.BlockSpec((rope_dim // 2, rows), lambda i: (0, 0)),
            pl.BlockSpec((hb, width, qrank), lambda i: (i, 0, 0)),
            pl.BlockSpec((rank, hb, nope), lambda i: (0, i, 0)),
        ],
        out_specs=pl.BlockSpec((rows, hb, rank + 128), lambda i: (0, i, 0)),
        out_shape=jax.ShapeDtypeStruct((rows, heads, rank + 128), jnp.bfloat16),
        scratch_shapes=[
            pltpu.VMEM((hb * width, rows), jnp.float32),
            pltpu.VMEM((rank * hb, nope), jnp.float32),
            pltpu.VMEM((rank // 128, rows * hb, 128), jnp.float32),
            pltpu.VMEM((rows * hb, 128), jnp.float32),
        ],
        compiler_params=pltpu.CompilerParams(dimension_semantics=("arbitrary",), vmem_limit_bytes=48 * 1024 * 1024),
        cost_estimate=pl.CostEstimate(flops=2 * rows * heads * (width * qrank + nope * rank), bytes_accessed=70_000_000, transcendentals=0),
        name="queries",
    )(cq, cos_w, sin_w, wq, w_uk)


def project_inputs(hidden, positions, w_dq, gain_q, w_dkv, gain_kv, w_uq, w_uk):
    kv_rank = w_uk.shape[0]
    nope_dim = w_uk.shape[2]
    cos_t, sin_t = rope_tables(positions, w_uq.shape[2] - nope_dim)
    h_q = jnp.dot(hidden, w_dq, preferred_element_type=jnp.float32).astype(jnp.bfloat16)
    c_q = rms_norm(h_q, gain_q).astype(jnp.bfloat16)
    query = queries(c_q, cos_t.T, sin_t.T, w_uq, w_uk)
    kv_down = jnp.dot(hidden, w_dkv, preferred_element_type=jnp.float32).astype(jnp.bfloat16)
    lat_new = rms_norm(kv_down[:, :kv_rank], gain_kv).astype(jnp.bfloat16)
    rope_new = rotate_pairs(kv_down[:, kv_rank:].astype(jnp.float32), cos_t, sin_t).astype(jnp.bfloat16)
    return query, lat_new, rope_new


def attend_kernel(score_scale, n_groups, first, n_alias, widths, perm, pos, base, query, lat_new, rope_new, lat_in, rope_in, *rest):
    (lat_out, rope_out, u_out, ml_out, lat_buf, rope_buf, u_buf,
     lat_rd, rope_rd, lat_wr, rope_wr, u_wr) = rest[n_alias:]
    g = pl.program_id(0)
    seq = lat_buf.shape[1]
    rank = lat_buf.shape[2]
    rope_dim = rope_buf.shape[1]
    heads = query.shape[1]
    start = base[0]
    rope_cols = rope_new[...].astype(jnp.float32).T

    def reads(group, slot, j):
        req = perm[first + group * GROUP + j]
        b = slot * GROUP + j
        return (pltpu.make_async_copy(lat_in.at[req], lat_buf.at[b], lat_rd.at[b]),
                pltpu.make_async_copy(rope_in.at[req], rope_buf.at[b], rope_rd.at[b]))

    def writes(group, slot, j):
        req = perm[first + group * GROUP + j]
        b = slot * GROUP + j
        return (pltpu.make_async_copy(lat_buf.at[b], lat_out.at[req], lat_wr.at[b]),
                pltpu.make_async_copy(rope_buf.at[b], rope_out.at[req], rope_wr.at[b]))

    lanes = u_buf.shape[1]

    def u_write(group, slot):
        return [pltpu.make_async_copy(u_buf.at[slot, q].reshape(heads, GROUP, 128),
                                      u_out.at[:, pl.ds(group * GROUP, GROUP), pl.ds(q * 128, 128)], u_wr.at[slot, q])
                for q in range(lanes)]

    @pl.when(g == 0)
    def _():
        ml_out[0] = jnp.full(ml_out.shape[1:], MASK_VALUE, jnp.float32)
        ml_out[1] = jnp.zeros(ml_out.shape[1:], jnp.float32)
        for a in range(AHEAD):
            for j in range(GROUP):
                for c in reads(a, a, j):
                    c.start()

    nxt = lax.rem(g + AHEAD, SETS)

    @pl.when(g >= SETS - AHEAD)
    def _():
        for j in range(GROUP):
            for c in writes(g - (SETS - AHEAD), nxt, j):
                c.wait()

    @pl.when(g + AHEAD < n_groups)
    def _():
        for j in range(GROUP):
            for c in reads(g + AHEAD, nxt, j):
                c.start()

    cur = lax.rem(g, SETS)
    uslot = lax.rem(g, 2)

    @pl.when(g >= 2)
    def _():
        for c in u_write(g - 2, uslot):
            c.wait()

    for j in range(GROUP):
        for c in reads(g, cur, j):
            c.wait()

    def update(j, _):
        local = pos[first + g * GROUP + j] - start
        b = cur * GROUP + j

        @pl.when((local >= 0) & (local < seq))
        def _():
            row0 = pl.multiple_of((local // 16) * 16, 16)
            rows = lat_buf[b, pl.ds(row0, 16), :].astype(jnp.float32)
            hit = lax.broadcasted_iota(jnp.int32, rows.shape, 0) == local - row0
            fresh = jnp.sum(jnp.where(lax.broadcasted_iota(jnp.int32, (GROUP, rank), 0) == j, lat_new[...].astype(jnp.float32), 0.0), axis=0, keepdims=True)
            lat_buf[b, pl.ds(row0, 16), :] = jnp.where(hit, fresh, rows).astype(lat_buf.dtype)
            col0 = pl.multiple_of((local // 128) * 128, 128)
            cols = rope_buf[b, :, pl.ds(col0, 128)].astype(jnp.float32)
            hit = lax.broadcasted_iota(jnp.int32, cols.shape, 1) == local - col0
            rope_buf[b, :, pl.ds(col0, 128)] = jnp.where(hit, jnp.sum(jnp.where(lax.broadcasted_iota(jnp.int32, rope_cols.shape, 1) == j, rope_cols, 0.0), axis=1, keepdims=True), cols).astype(rope_buf.dtype)
        return 0

    lax.fori_loop(0, GROUP, update, 0)

    span = pos[first + g * GROUP] - start + 1

    def compute(width):
        lane = lax.broadcasted_iota(jnp.int32, (heads, 128), 1)
        half = g * GROUP // 128
        m_all = ml_out[0, half]
        l_all = ml_out[1, half]
        slots = lax.broadcasted_iota(jnp.int32, (heads, width), 1)

        def scores(j):
            b = cur * GROUP + j
            s = lax.dot_general(query[j, :, :rank], lat_buf[b, :width, :], (((1,), (1,)), ((), ())), preferred_element_type=jnp.float32)
            return s + jnp.dot(query[j, :, rank:rank + rope_dim], rope_buf[b, :, :width], preferred_element_type=jnp.float32)

        def several(t, carry):
            m_all, l_all = carry
            s_next = scores(t * UNROLL)
            for jj in range(UNROLL):
                j = t * UNROLL + jj
                s = s_next * score_scale
                if jj + 1 < UNROLL:
                    s_next = scores(j + 1)
                i = g * GROUP + j
                valid = slots <= pos[first + i] - start
                s = jnp.where(valid, s, MASK_VALUE)
                m = jnp.max(s, axis=1, keepdims=True)
                w = jnp.where(valid, jnp.exp(s - m), 0.0)
                l = jnp.sum(w, axis=1, keepdims=True)
                u = jnp.dot(w.astype(jnp.bfloat16), lat_buf[cur * GROUP + j, :width, :], preferred_element_type=jnp.float32)
                for q in range(lanes):
                    u_buf[uslot, q, pl.ds(j, heads, stride=GROUP), :] = u[:, q * 128:(q + 1) * 128]
                here = lane == i - half * 128
                m_all = jnp.where(here, m, m_all)
                l_all = jnp.where(here, l, l_all)
            return m_all, l_all

        m_all, l_all = lax.fori_loop(0, GROUP // UNROLL, several, (m_all, l_all))
        ml_out[0, half] = m_all
        ml_out[1, half] = l_all

    low = 0
    for width in widths:
        cond = span > low if width == seq else (span > low) & (span <= width)

        @pl.when(cond)
        def _(width=width):
            compute(width)
        low = width

    @pl.when(span <= 0)
    def _():
        u_buf[uslot] = jnp.zeros(u_buf.shape[1:], jnp.float32)

    for j in range(GROUP):
        for c in writes(g, cur, j):
            c.start()
    for c in u_write(g, uslot):
        c.start()

    @pl.when(g == n_groups - 1)
    def _():
        for k in range(SETS - AHEAD):
            for j in range(GROUP):
                for c in writes(g - k, lax.rem(g - k, SETS), j):
                    c.wait()
        for k in range(2):
            for c in u_write(g - k, lax.rem(g - k, 2)):
                c.wait()


def attend(first, count, done, perm, pos, base, query, lat_new, rope_new, lat_cache, rope_t, score_scale):
    heads = query.shape[1]
    rank = lat_cache.shape[2]
    seq = lat_cache.shape[1]
    rope_dim = rope_t.shape[1]
    n_groups = count // GROUP
    g0 = first // GROUP
    n_ml = pl.cdiv(count, 128)
    any_spec = pl.BlockSpec(memory_space=pl.ANY)
    return pl.pallas_call(
        functools.partial(attend_kernel, score_scale, n_groups, first, len(done), (128, seq) if first or count == perm.shape[0] else (seq,)),
        grid_spec=pltpu.PrefetchScalarGridSpec(
            num_scalar_prefetch=3,
            grid=(n_groups,),
            in_specs=[
                pl.BlockSpec((GROUP, heads, query.shape[2]), lambda g, *_: (g + g0, 0, 0)),
                pl.BlockSpec((GROUP, rank), lambda g, *_: (g + g0, 0)),
                pl.BlockSpec((GROUP, rope_dim), lambda g, *_: (g + g0, 0)),
            ] + [any_spec] * (2 + len(done)),
            out_specs=[any_spec, any_spec, any_spec,
                       pl.BlockSpec((2, n_ml, heads, 128), lambda g, *_: (0, 0, 0, 0))],
            scratch_shapes=[
                pltpu.VMEM((SETS * GROUP, seq, rank), jnp.bfloat16),
                pltpu.VMEM((SETS * GROUP, rope_dim, seq), jnp.bfloat16),
                pltpu.VMEM((2, rank // 128, heads * GROUP, 128), jnp.float32),
                pltpu.SemaphoreType.DMA((SETS * GROUP,)),
                pltpu.SemaphoreType.DMA((SETS * GROUP,)),
                pltpu.SemaphoreType.DMA((SETS * GROUP,)),
                pltpu.SemaphoreType.DMA((SETS * GROUP,)),
                pltpu.SemaphoreType.DMA((2, rank // 128)),
            ],
        ),
        out_shape=[
            jax.ShapeDtypeStruct(lat_cache.shape, lat_cache.dtype),
            jax.ShapeDtypeStruct(rope_t.shape, rope_t.dtype),
            jax.ShapeDtypeStruct((heads, count, rank), jnp.float32),
            jax.ShapeDtypeStruct((2, n_ml, heads, 128), jnp.float32),
        ],
        input_output_aliases={8: 0, 9: 1} if done else {},
        compiler_params=pltpu.CompilerParams(dimension_semantics=("arbitrary",), vmem_limit_bytes=48 * 1024 * 1024),
        cost_estimate=pl.CostEstimate(flops=16 * count * heads * seq * (2 * rank + rope_dim), bytes_accessed=count * seq * rank * 5,
                                      transcendentals=0),
        name=f"attend{first}_{count}",
    )(perm, pos, base, query, lat_new, rope_new, lat_cache, rope_t, *done)


CH = 4


def row_block(rows):
    return max(d for d in range(8, 65, 8) if rows % d == 0)


def remote(src, dst, ss, rs, dev):
    return pltpu.make_async_remote_copy(src_ref=src, dst_ref=dst, send_sem=ss, recv_sem=rs,
                                        device_id=dev, device_id_type=MESH)


def factors(stats, mine, other, lo, count, f_buf):
    sources = stats.shape[0]
    for b in range(stats.shape[2]):
        m = [stats[s, 0, b, pl.ds(lo, count), :] for s in range(sources)]
        top = functools.reduce(jnp.maximum, m)
        total = sum(jnp.exp(m[s] - top) * stats[s, 1, b, pl.ds(lo, count), :] for s in range(sources))
        total = jnp.maximum(total, 1e-30)
        for slot, s in enumerate((mine, other)):
            f = jnp.exp(stats[s, 0, b, pl.ds(lo, count), :] - top) / total
            f_buf[slot, b * 128:(b + 1) * 128, :] = f.T


def column(f_buf, slot, r0, rb, h):
    f = f_buf[slot, pl.ds(r0, rb), :]
    lane = lax.broadcasted_iota(jnp.int32, f.shape, 1)
    return jnp.sum(jnp.where(lane == h, f, 0.0), axis=1, keepdims=True)


def pair_kernel(u_ref, ml_ref, keep_ref, give_ref, d_buf, own_buf, stats, f_buf,
                d_ss, d_rs, s_ss, s_rs, own_sem, out_sem):
    hh, rows, rank = d_buf.shape
    half = rows // 2
    n_chunk = hh // CH
    dp = lax.axis_index('dp')
    tp = lax.axis_index('tp')
    sp = lax.axis_index('sp')
    n_sp = stats.shape[0]
    core = lax.rem(sp, 2)
    x = sp // 2
    mate = x * 2 + (1 - core)
    peers = [lax.rem(sp + i, n_sp) for i in range(1, n_sp)]
    barrier = pltpu.get_barrier_semaphore()
    for p in peers:
        pl.semaphore_signal(barrier, inc=1, device_id={'dp': dp, 'tp': tp, 'sp': p}, device_id_type=MESH)

    def own_load(k):
        return pltpu.make_async_copy(u_ref.at[pl.ds(core * hh + k * CH, CH)], own_buf.at[lax.rem(k, 2)], own_sem.at[lax.rem(k, 2)])

    for k in range(2):
        own_load(k).start()
    pl.semaphore_wait(barrier, n_sp - 1)

    def stat_send(i):
        return remote(ml_ref, stats.at[sp], s_ss.at[i], s_rs.at[sp], {'dp': dp, 'tp': tp, 'sp': peers[i]})

    def stat_recv(i):
        return remote(ml_ref, stats.at[peers[i]], s_ss.at[i], s_rs.at[peers[i]], {'dp': dp, 'tp': tp, 'sp': peers[i]})

    def d_copy(k):
        return remote(u_ref.at[pl.ds((1 - core) * hh + k * CH, CH)], d_buf.at[pl.ds(k * CH, CH)],
                      d_ss.at[k], d_rs.at[k], {'dp': dp, 'tp': tp, 'sp': mate})

    for i in range(n_sp - 1):
        stat_send(i).start()
    for k in range(n_chunk):
        d_copy(k).start()
    stats[sp] = ml_ref[...]
    for i in range(n_sp - 1):
        stat_recv(i).wait_recv()
    factors(stats, sp, mate, pl.multiple_of(core * hh, 8), hh, f_buf)

    keep = pl.multiple_of(x * half, 8)
    give = pl.multiple_of((1 - x) * half, 8)
    rb = row_block(rows)

    def outs(k):
        hs = pl.ds(k * CH, CH)
        return (pltpu.make_async_copy(d_buf.at[hs, pl.ds(keep, half), :], keep_ref.at[hs], out_sem.at[0, k]),
                pltpu.make_async_copy(d_buf.at[hs, pl.ds(give, half), :], give_ref.at[hs], out_sem.at[1, k]))

    def chunk(k, _):
        own_load(k).wait()
        d_copy(k).wait_recv()
        slot = lax.rem(k, 2)

        def scale(t, _):
            a = t // (rows // rb)
            r0 = pl.multiple_of(lax.rem(t, rows // rb) * rb, rb)
            h = k * CH + a
            fo = column(f_buf, 0, r0, rb, h)
            fm = column(f_buf, 1, r0, rb, h)
            d_buf[h, pl.ds(r0, rb), :] = fo * own_buf[slot, a, pl.ds(r0, rb), :] + fm * d_buf[h, pl.ds(r0, rb), :]
            return 0

        lax.fori_loop(0, CH * (rows // rb), scale, 0)
        for c in outs(k):
            c.start()

        @pl.when(k + 2 < n_chunk)
        def _():
            own_load(k + 2).start()
        return 0

    lax.fori_loop(0, n_chunk, chunk, 0)
    for i in range(n_sp - 1):
        stat_send(i).wait_send()

    def drain(k, _):
        d_copy(k).wait_send()
        for c in outs(k):
            c.wait()
        return 0

    lax.fori_loop(0, n_chunk, drain, 0)


def pair_reduce(cid, n_sp, u, ml):
    heads, rows, rank = u.shape
    hh = heads // 2
    n_chunk = hh // CH
    dma = pltpu.SemaphoreType.DMA
    any_spec = pl.BlockSpec(memory_space=pl.ANY)
    return pl.pallas_call(
        pair_kernel,
        in_specs=[any_spec, pl.BlockSpec(memory_space=pltpu.VMEM)],
        out_specs=[any_spec, any_spec],
        out_shape=[jax.ShapeDtypeStruct((hh, rows // 2, rank), jnp.float32)] * 2,
        scratch_shapes=[
            pltpu.VMEM((hh, rows, rank), jnp.float32),
            pltpu.VMEM((2, CH, rows, rank), jnp.float32),
            pltpu.VMEM((n_sp,) + ml.shape, jnp.float32),
            pltpu.VMEM((2, ml.shape[1] * 128, hh), jnp.float32),
            dma((n_chunk,)), dma((n_chunk,)), dma((n_sp,)), dma((n_sp,)), dma((2,)), dma((2, n_chunk)),
        ],
        compiler_params=pltpu.CompilerParams(collective_id=cid, has_side_effects=True, vmem_limit_bytes=48 * 1024 * 1024),
        cost_estimate=pl.CostEstimate(flops=2_000_000_000, bytes_accessed=20_000_000, transcendentals=0),
        name=f"pair{rows}",
    )(u, ml)


def combine_kernel(n_rest, keep_ref, got_ref, wuv_ref, wout_ref, hid_ref, sel_ref, sel_t_ref, *refs):
    if n_rest:
        u_ref, ml_ref = refs[:2]
        refs = refs[2:]
    (out_ref, att, hid_buf, out_buf, hid_sem, out_sem, keep_buf, got_buf, o_out, o_in, o_all, w_buf, p_buf, y_buf, wuv_buf, k_buf,
     o_ss, o_rs, y_ss, y_rs, h_ss, h_rs, c_ss, c_rs, w_ss, w_rs,
     own_sem, keep_sem, wt_sem, wuv_sem) = refs[:30]
    if n_rest:
        d_buf, own_buf, stats, f_buf, d_ss, d_rs, s_ss, s_rs = refs[30:]
    hh, half, rank = keep_ref.shape
    r_own = half + n_rest
    vdim = wuv_buf.shape[3]
    wh = wuv_buf.shape[2]
    n_chunk = hh // CH
    n_blk, _, bcol = p_buf.shape
    dp = lax.axis_index('dp')
    tp = lax.axis_index('tp')
    sp = lax.axis_index('sp')
    core = lax.rem(sp, 2)
    x = sp // 2
    to_mate = {'dp': dp, 'tp': tp, 'sp': x * 2 + (1 - core)}
    to_x = {'dp': dp, 'tp': tp, 'sp': (1 - x) * 2 + core}
    to_y = {'dp': dp, 'tp': 1 - tp, 'sp': sp}

    barrier = pltpu.get_barrier_semaphore()
    for dev in (to_mate, to_x, to_y):
        pl.semaphore_signal(barrier, inc=1, device_id=dev, device_id_type=MESH)

    def loads(k):
        slot = lax.rem(k, 2)
        hs = pl.ds(k * CH, CH)
        cs = [pltpu.make_async_copy(keep_ref.at[hs], keep_buf.at[slot], keep_sem.at[0, slot]),
              pltpu.make_async_copy(got_ref.at[hs], got_buf.at[slot], keep_sem.at[1, slot])]
        if n_rest:
            cs.append(pltpu.make_async_copy(u_ref.at[pl.ds(core * hh + k * CH, CH)], own_buf.at[slot], own_sem.at[slot]))
        return cs

    def w_load(j):
        col = pl.multiple_of(core * (n_blk * bcol) + j * bcol, 128)
        return pltpu.make_async_copy(wout_ref.at[:, pl.ds(col, bcol)], w_buf.at[lax.rem(j, 2)], wt_sem.at[lax.rem(j, 2)])

    for k in range(2):
        for c in loads(k):
            c.start()

    def wuv_load(a):
        return pltpu.make_async_copy(wuv_ref.at[:, pl.ds(core * hh + a * wh, wh), :], wuv_buf.at[a], wuv_sem.at[a])

    for a in range(hh // wh):
        wuv_load(a).start()
    pl.semaphore_wait(barrier, 3)

    def d_copy(k):
        return remote(u_ref.at[pl.ds((1 - core) * hh + k * CH, CH)], d_buf.at[pl.ds(k * CH, CH)],
                      d_ss.at[k], d_rs.at[k], to_mate)

    if n_rest:
        stat_copy = remote(ml_ref, stats.at[1], s_ss, s_rs, to_mate)
        stat_copy.start()
        for k in range(n_chunk):
            d_copy(k).start()
    for j in range(2):
        w_load(j).start()
    if n_rest:
        stats[0] = ml_ref[...]
        stat_copy.wait_recv()
        factors(stats, 0, 1, pl.multiple_of(core * hh, 8), hh, f_buf)

    def o_copy(k):
        return remote(o_out.at[pl.ds(k * CH, CH)], o_in.at[pl.ds(k * CH, CH)], o_ss.at[k], o_rs.at[k], to_mate)

    rb = row_block(n_rest) if n_rest else 8

    def project_chunk(k, _):
        slot = lax.rem(k, 2)
        for c in loads(k):
            c.wait()
        if n_rest:
            d_copy(k).wait_recv()

            def scale(t, _):
                a = t // (n_rest // rb)
                r0 = pl.multiple_of(lax.rem(t, n_rest // rb) * rb, rb)
                h = k * CH + a
                fo = column(f_buf, 0, r0, rb, h)
                fm = column(f_buf, 1, r0, rb, h)
                d_buf[h, pl.ds(r0, rb), :] = fo * own_buf[slot, a, pl.ds(r0, rb), :] + fm * d_buf[h, pl.ds(r0, rb), :]
                return 0

            lax.fori_loop(0, CH * (n_rest // rb), scale, 0)

        @pl.when(lax.rem(k, wh // CH) == 0)
        def _():
            wuv_load(k // (wh // CH)).wait()
            k_buf[...] = wuv_buf[k // (wh // CH)].astype(jnp.float32).reshape(k_buf.shape)

        def project(a, _):
            h = k * CH + a
            wuv_h = k_buf[pl.ds(lax.rem(h, wh), rank, stride=wh), :].astype(jnp.bfloat16)
            u = keep_buf[slot, a] + got_buf[slot, a]
            if n_rest:
                u = jnp.concatenate([u, d_buf[h]], axis=0)
            o = jnp.dot(u.astype(jnp.bfloat16), wuv_h, preferred_element_type=jnp.float32).astype(jnp.bfloat16)
            o_all[:, pl.ds(pl.multiple_of((core * hh + h) * vdim, 128), vdim)] = o
            o_out[h] = o.astype(jnp.float32)
            return 0

        lax.fori_loop(0, CH, project, 0)
        o_copy(k).start()

        @pl.when(k + 2 < n_chunk)
        def _():
            for c in loads(k + 2):
                c.start()
        return 0

    lax.fori_loop(0, n_chunk, project_chunk, 0)

    def place_chunk(k, _):
        o_copy(k).wait_recv()

        def place(a, _):
            h = k * CH + a
            o_all[:, pl.ds(pl.multiple_of(((1 - core) * hh + h) * vdim, 128), vdim)] = o_in[h].astype(jnp.bfloat16)
            return 0

        lax.fori_loop(0, CH, place, 0)
        return 0

    lax.fori_loop(0, n_chunk, place_chunk, 0)

    mine = core * n_blk
    theirs = (1 - core) * n_blk

    def y_copy(j):
        return remote(p_buf.at[j], y_buf.at[j], y_ss.at[j], y_rs.at[j], to_y)

    def c_copy(j):
        return remote(att.at[x, mine + j], att.at[x, mine + j], c_ss.at[j], c_rs.at[j], to_mate)

    def h_copy(j):
        return remote(att.at[x, mine + j], att.at[x, mine + j], h_ss.at[j], h_rs.at[j], to_x)

    def w_copy(j):
        return remote(att.at[1 - x, mine + j], att.at[1 - x, mine + j], w_ss.at[j], w_rs.at[j], to_mate)

    def hid_load(kind, j):
        col = pl.multiple_of(((theirs if kind else mine) + j) * bcol, 128)
        slot = 2 * kind + lax.rem(j, 2)
        return pltpu.make_async_copy(hid_ref.at[:, pl.ds(col, bcol)], hid_buf.at[slot], hid_sem.at[slot])

    def out_store(kind, j):
        col = pl.multiple_of(((theirs if kind else mine) + j) * bcol, 128)
        slot = 2 * kind + lax.rem(j, 2)
        return pltpu.make_async_copy(out_buf.at[slot], out_ref.at[:, pl.ds(col, bcol)], out_sem.at[slot])

    def total(j):
        y_copy(j).wait_recv()
        att[x, mine + j] = y_buf[j] + p_buf[j]
        h_copy(j).start()
        c_copy(j).start()

    def forward(j):
        h_copy(j).wait_recv()
        w_copy(j).start()

    def finalize(kind, j):
        slot = 2 * kind + lax.rem(j, 2)
        blk = (theirs if kind else mine) + j
        hid_load(kind, j).wait()
        hid = jnp.dot(sel_ref[...], hid_buf[slot], preferred_element_type=jnp.float32)
        parts = [att[0, blk, :half], att[1, blk, :half]]
        if n_rest:
            parts.append(att[0, blk, half:])
        rows_s = (hid + jnp.concatenate(parts, axis=0)).astype(jnp.bfloat16)

        @pl.when(j >= 2)
        def _():
            out_store(kind, j - 2).wait()

        out_buf[slot] = jnp.dot(sel_t_ref[...], rows_s, preferred_element_type=jnp.float32).astype(out_buf.dtype)
        out_store(kind, j).start()

        @pl.when(j + 2 < n_blk)
        def _():
            hid_load(kind, j + 2).start()

    def finalize_mate(j):
        pltpu.make_async_remote_copy(src_ref=att.at[x, theirs + j], dst_ref=att.at[x, theirs + j], send_sem=c_ss.at[j],
                                     recv_sem=c_rs.at[j], device_id=to_mate, device_id_type=MESH).wait_recv()
        pltpu.make_async_remote_copy(src_ref=att.at[1 - x, theirs + j], dst_ref=att.at[1 - x, theirs + j], send_sem=w_ss.at[j],
                                     recv_sem=w_rs.at[j], device_id=to_mate, device_id_type=MESH).wait_recv()
        finalize(1, j)

    for kind in range(2):
        for j in range(2):
            hid_load(kind, j).start()
    early = (4, 8, 11)
    lag = len(early)

    def block(j, _):
        w_load(j).wait()
        p_buf[j] = jnp.dot(o_all[...], w_buf[lax.rem(j, 2)], preferred_element_type=jnp.float32)
        y_copy(j).start()

        @pl.when(j + 2 < n_blk)
        def _():
            w_load(j + 2).start()

        for i, at in enumerate(early):
            @pl.when(j == at)
            def _(i=i):
                total(i)
        return 0

    lax.fori_loop(0, n_blk, block, 0)

    def finish(j, _):
        @pl.when(j < n_blk)
        def _():
            total(j)

        @pl.when(j - lag < n_blk)
        def _():
            forward(j - lag)
            finalize(0, j - lag)

        @pl.when(j - lag >= 1)
        def _():
            finalize_mate(j - lag - 1)
        return 0

    lax.fori_loop(lag, n_blk + lag + 1, finish, 0)

    def drain(k, _):
        if n_rest:
            d_copy(k).wait_send()
        o_copy(k).wait_send()
        return 0

    lax.fori_loop(0, n_chunk, drain, 0)
    if n_rest:
        stat_copy.wait_send()

    def drain_blocks(j, _):
        y_copy(j).wait_send()
        h_copy(j).wait_send()
        c_copy(j).wait_send()
        w_copy(j).wait_send()
        return 0

    lax.fori_loop(0, n_blk, drain_blocks, 0)
    for kind in range(2):
        for j in range(n_blk - 2, n_blk):
            out_store(kind, j).wait()


def combine(cid, keep, got, wuv, wout, hidden, sel, sel_t, rest):
    hh, half, rank = keep.shape
    n_rest = rest[0].shape[1] if rest else 0
    vdim = wuv.shape[2]
    depth, width = wout.shape
    r_own = half + n_rest
    bcol = 256
    n_blk = width // 2 // bcol
    n_chunk = hh // CH
    dma = pltpu.SemaphoreType.DMA
    any_spec = pl.BlockSpec(memory_space=pl.ANY)
    vmem_spec = pl.BlockSpec(memory_space=pltpu.VMEM)
    rows = hidden.shape[0]
    scratch = [
        pltpu.VMEM((2, 2 * n_blk, r_own, bcol), jnp.float32),
        pltpu.VMEM((4, rows, bcol), jnp.bfloat16),
        pltpu.VMEM((4, rows, bcol), jnp.bfloat16),
        dma((4,)), dma((4,)),
        pltpu.VMEM((2, CH, half, rank), jnp.float32),
        pltpu.VMEM((2, CH, half, rank), jnp.float32),
        pltpu.VMEM((hh, r_own, vdim), jnp.float32),
        pltpu.VMEM((hh, r_own, vdim), jnp.float32),
        pltpu.VMEM((r_own, depth), jnp.bfloat16),
        pltpu.VMEM((2, depth, bcol), jnp.bfloat16),
        pltpu.VMEM((n_blk, r_own, bcol), jnp.float32),
        pltpu.VMEM((n_blk, r_own, bcol), jnp.float32),
        pltpu.VMEM((hh // 8, rank, 8, vdim), jnp.bfloat16),
        pltpu.VMEM((rank * 8, vdim), jnp.float32),
    ] + [dma((n_chunk,))] * 2 + [dma((n_blk,))] * 8 + [dma((2,)), dma((2, 2)), dma((2,)), dma((hh // 8,))]
    if rest:
        scratch += [
            pltpu.VMEM((hh, n_rest, rank), jnp.float32),
            pltpu.VMEM((2, CH, n_rest, rank), jnp.float32),
            pltpu.VMEM((2,) + rest[1].shape, jnp.float32),
            pltpu.VMEM((2, rest[1].shape[1] * 128, hh), jnp.float32),
            dma((n_chunk,)), dma((n_chunk,)), dma(()), dma(()),
        ]
    return pl.pallas_call(
        functools.partial(combine_kernel, n_rest),
        in_specs=[any_spec] * 5 + [vmem_spec, vmem_spec] + ([any_spec, vmem_spec] if rest else []),
        out_specs=any_spec,
        out_shape=jax.ShapeDtypeStruct(hidden.shape, hidden.dtype),
        scratch_shapes=scratch,
        compiler_params=pltpu.CompilerParams(collective_id=cid, has_side_effects=True, vmem_limit_bytes=VMEM_LIMIT),
        name=f"combine{2 * half}",
    )(keep, got, wuv, wout, hidden, sel, sel_t, *rest)


def solution(mesh):
    row_spec = P('dp', None)
    cache_spec = P('dp', 'sp', None)
    head_spec = P(None, 'tp', None)
    in_specs = (row_spec, cache_spec, cache_spec, P('dp'), P(), P(), P(), P(), head_spec, head_spec, head_spec, P('tp', None))
    out_specs = (row_spec, cache_spec, cache_spec)
    n_sp = mesh.shape['sp']

    def local_step(hidden, lat_cache, rope_cache, positions, w_dq, gain_q, w_dkv, gain_kv, w_uq, w_uk, w_uv, w_out):
        rows = hidden.shape[0]
        seq = lat_cache.shape[1]
        heads = w_uk.shape[1]
        score_scale = YARN_MSCALE ** 2 / math.sqrt(w_uq.shape[2])
        sp = lax.axis_index('sp')

        idx = jnp.arange(rows)
        before = (positions[None, :] > positions[:, None]) | ((positions[None, :] == positions[:, None]) & (idx[None, :] < idx[:, None]))
        rank = jnp.sum(before.astype(jnp.int32), axis=1)
        sel = rank[None, :] == idx[:, None]
        perm = jnp.sum(jnp.where(sel, idx[None, :], 0), axis=1).astype(jnp.int32)
        pos_s = jnp.sum(jnp.where(sel, positions[None, :], 0), axis=1).astype(jnp.int32)
        sel16 = sel.astype(jnp.bfloat16)
        hidden_s = jnp.dot(sel16, hidden, preferred_element_type=jnp.float32).astype(jnp.bfloat16)

        query, lat_new, rope_new = project_inputs(hidden_s, pos_s, w_dq, gain_q, w_dkv, gain_kv, w_uq, w_uk)
        base = (sp * seq).astype(jnp.int32).reshape(1)
        rope_t = rope_cache.transpose(0, 2, 1)
        n_over = jnp.sum((positions >= (n_sp // 2) * seq).astype(jnp.int32))
        sizes = sorted({min(rows, max(16, s * rows // 256)) for s in SIZES})
        which = sum((n_over > s).astype(jnp.int32) for s in sizes[:-1])
        swap = [(i, (i + n_sp // 2) % n_sp) for i in range(n_sp)]

        def branch(n_cross, cid):
            def run(perm, pos_s, base, query, lat_new, rope_new, lat_cache, rope_t, w_uv, w_out, hidden, sel16):
                common = (perm, pos_s, base, query, lat_new, rope_new, lat_cache, rope_t, score_scale)
                lat_out, rope_out, u_first, ml_first = attend(0, n_cross, (), *common)
                keep, give = pair_reduce(2 * cid, n_sp, u_first, ml_first)
                got = lax.ppermute(give, 'sp', swap)
                rest = ()
                if n_cross < rows:
                    lat_out, rope_out, *rest = attend(n_cross, rows - n_cross, (lat_out, rope_out), *common)
                out = combine(2 * cid + 1, keep, got, w_uv, w_out, hidden, sel16, sel16.T, rest)
                return out, lat_out, rope_out
            return run

        out, lat_out, rope_out = lax.switch(which, [branch(s, i) for i, s in enumerate(sizes)], perm, pos_s, base, query,
                                            lat_new, rope_new, lat_cache, rope_t, w_uv, w_out, hidden, sel16)
        return out, lat_out, rope_out.transpose(0, 2, 1)

    return jax.shard_map(local_step, mesh=mesh, in_specs=in_specs, out_specs=out_specs, check_vma=False)
```

profile of v0, /device:TPU:0, one launch (start us, length us, event | category | flops | bytes accessed | tf_op | source)
XLA Modules:
  0.0 319.6 jit_solution(14136186075066919990)
XLA Ops:
  0.6 1.3 fusion.16
  3.3 0.9 convert_reduce_fusion
  4.1 0.7 convert_element_type.75
  4.8 0.8 select_reduce_fusion
  5.7 0.7 convert_element_type.69
  6.4 0.2 multiply_sine_fusion.1
  6.6 0.8 fusion.4
  7.3 3.3 %convolution_convert_fusion = bf16[256,7168]{1,0:T(8,128)(2,1)S(1)} fusion(bf16[256,7168]{1,0:T(8,128)(2,1)} %param.15, s32[256]{0:T(256)S(1)} %convert_reduce_fusion), kind=kOutput, calls=%fused_computation | convolution fusion | flops 941424640 | bytes 7341056 | tf_op jit(solution)/shard_map/dot_general | solution.py:781
  10.6 5.7 %convolution_convert_fusion.2 = bf16[256,576]{0,1:T(8,128)(2,1)S(1)} fusion(bf16[256,7168]{1,0:T(8,128)(2,1)S(1)} %convolution_convert_fusion, bf16[7168,576]{0,1:T(8,128)(2,1)} %param.21), kind=kOutput, calls=%fused_computation.5 | convolution fusion | flops 2114076672 | bytes 12222464 | tf_op jit(solution)/shard_map/dot_general | solution.py:106
  16.3 10.4 %multiply_reduce_fusion = (f32[256]{0:T(256)S(1)}, f32[256,1536]{1,0:T(8,128)S(1)}) fusion(bf16[256,7168]{1,0:T(8,128)(2,1)S(1)} %convolution_convert_fusion, bf16[7168,1536]{1,0:T(8,128)(2,1)} %param.19), kind=kOutput, calls=%fused_computation.4 | convolution fusion | flops 5638717440 | bytes 27264000 | tf_op jit(solution)/shard_map/dot_general | solution.py:103
  26.7 0.2 multiply_convert_fusion.cq
  26.9 0.1 fusion.1
  27.0 0.1 fusion.3
  27.1 0.2 fusion.13
  27.3 32.4 %queries.1 = bf16[256,64,640]{2,1,0:T(8,128)(2,1)} custom-call(bf16[256,1536]{1,0:T(8,128)(2,1)S(1)} %multiply_convert_fusion.cq, f32[32,256]{1,0:T(8,128)S(1)} %get-tuple-element.184.cos_t, f32[32,256]{1,0:T(8,128)S(1)} %get-tuple-element.183.sin_t, bf16[64,192,1536]{2,1,0:T(8,128)(2,1)} %bitcast.12, bf16[512,64,128]{2,1,0:T(8,128)(2,1)} %wk.1), custom_call_target="tpu_custom_call" | custom-call | flops 11811160064 | bytes 70000000 | tf_op jit(solution)/shard_map/queries/pallas_call | solution.py:75
  59.7 255.8 %conditional.1 = (bf16[256,7168]{1,0:T(8,128)(2,1)}, bf16[256,512,512]{2,1,0:T(8,128)(2,1)}, bf16[256,64,512]{2,1,0:T(8,128)(2,1)}) conditional(s32[]{:T(128)} %clamp.3, (s32[256]{0:T(256)S(1)}, s32[256]{0:T(256)S(1)}, s32[1]{0:T(128)}, bf16[256,64,640]{2,1,0:T(8,128)(2,1)}, bf16[256,512]{0,1:T(8,128)(2,1)S(1)}, ...), branch_computations={%region_6.7_spmd, %region_7.8_spmd, %region_8.9_spmd} | conditional | flops 148028882944 | bytes 390475104 | solution.py:804
  59.7 0.1 copy.23.rope_new
  59.8 0.1 copy.22.lat_new
  60.0 49.1 %attend0_96.1 = (bf16[256,512,512]{2,1,0:T(8,128)(2,1)}, bf16[256,64,512]{2,1,0:T(8,128)(2,1)}, f32[64,96,512]{2,1,0:T(8,128)}, f32[2,1,64,128]{3,2,1,0:T(8,128)S(1)}) custom-call(s32[256]{0:T(256)S(1)} %get-tuple-element.72.perm, s32[256]{0:T(256)S(1)} %get-tuple-element.73.pos, s32[1]{0:T(128)} %get-tuple-element.74.base, ...), custom_call_target="tpu_custom_call" | custom-call | flops 54760833024 | bytes 125829120 | tf_op jit(solution)/shard_map/cond/branch_0_fun/attend0_96/pallas_call | solution.py:275
  109.1 16.8 %pair96.1 = (f32[32,48,512]{2,1,0:T(8,128)S(1)}, f32[32,48,512]{2,1,0:T(8,128)}) custom-call(f32[64,96,512]{2,1,0:T(8,128)} %get-tuple-element.80.u_ref, f32[2,1,64,128]{3,2,1,0:T(8,128)S(1)} %get-tuple-element.81.ml_ref), custom_call_target="tpu_custom_call" | custom-call | flops 2000000000 | bytes 20000000 | tf_op jit(solution)/shard_map/cond/branch_0_fun/pair96/pallas_call | solution.py:436
  125.9 0.0 copy-start.1
  125.9 1.7 copy-done.1
  127.6 2.0 collective-permute-start
  129.6 0.0 copy-start.4
  129.6 77.7 %attend96_160.1 = (bf16[256,512,512]{2,1,0:T(8,128)(2,1)}, bf16[256,64,512]{2,1,0:T(8,128)(2,1)}, f32[64,160,512]{2,1,0:T(8,128)}, f32[2,2,64,128]{3,2,1,0:T(8,128)S(1)}) custom-call(s32[256]{0:T(256)S(1)} %get-tuple-element.72.perm, s32[256]{0:T(256)S(1)} %get-tuple-element.73.pos, ...), custom_call_target="tpu_custom_call", output_to_operand_aliasing={{0}: (8, {}), {1}: (9, {})} | custom-call | flops 91268055040 | bytes 209715200 | tf_op jit(solution)/shard_map/cond/branch_0_fun/attend96_160/pallas_call | solution.py:275
  207.3 0.0 copy-start.2
  207.3 0.6 copy-done.2
  208.0 0.0 copy-done.4
  208.0 0.8 copy.19.sel_ref
  208.7 0.0 collective-permute-done.got_ref
  208.7 106.8 %combine96.1 = bf16[256,7168]{1,0:T(8,128)(2,1)} custom-call(f32[32,48,512]{2,1,0:T(8,128)} %copy-done.1, f32[32,48,512]{2,1,0:T(8,128)} %collective-permute-done.got_ref, bf16[512,64,128]{2,1,0:T(8,128)(2,1)} %get-tuple-element.84.wuv_ref, bf16[8192,7168]{1,0:T(8,128)(2,1)} %get-tuple-element.85.wout_ref, bf16[256,7168]{1,0:T(8,128)(2,1)} %get-tuple-element.86.hid_ref, ...), custom_call_target="tpu_custom_call" | custom-call | tf_op jit(solution)/shard_map/cond/branch_0_fun/combine96/pallas_call | solution.py:748
  315.5 4.1 %copy.42 = bf16[256,7168]{1,0:T(8,128)(2,1)} copy(bf16[256,7168]{1,0:T(8,128)(2,1)} %get-tuple-element.199) | data formatting | bytes 7340032
  (6 shorter events, 0.0 us)
Async XLA Ops:
  125.9 1.7 copy-start.1
  127.6 81.2 %collective-permute-start = (f32[32,48,512]{2,1,0:T(8,128)}, f32[32,48,512]{2,1,0:T(8,128)}, u32[]{:S(2)}, u32[]{:S(2)}) collective-permute-start(f32[32,48,512]{2,1,0:T(8,128)} %get-tuple-element.83), channel_id=1, source_target_pairs={{0,2},{1,3},{2,0},{3,1},{4,6},{5,7},{6,4},{7,5}} | collective-permute-start | bytes 9437192 | tf_op jit(solution)/shard_map/cond/branch_0_fun/ppermute | solution.py:796
  129.6 78.4 %copy-start.4 = (bf16[256,256]{0,1:T(8,128)(2,1)S(1)}, bf16[256,256]{0,1:T(8,128)(2,1)}, u32[]{:S(2)}) copy-start(bf16[256,256]{0,1:T(8,128)(2,1)} %get-tuple-element.87) | copy-start | bytes 393220 | tf_op jit(solution)/shard_map/cond
  207.3 0.6 copy-start.2
where the time goes:
time: 320 us
  Pallas kernels  283 us (88%)
  matrix products  19.3 us (6%)
  local copies, waits for them, and re-layouts  7.42 us (2%)
  other arithmetic  6.01 us (2%)
    pallas_call x2, Pallas kernels, attend(): pl.pallas_call(functools.partial(attend_kernel, score_scale, n_groups, fi...  127 us
    pallas_call x1, Pallas kernels, combine(): pl.pallas_call(functools.partial(combine_kernel, n_rest), in_specs=[any_s...  107 us
    pallas_call x1, Pallas kernels, queries(): pl.pallas_call(query_kernel, grid=(heads // hb,), in_specs=[pl.BlockSpec(...  32.4 us
    pallas_call x1, Pallas kernels, pair_reduce(): pl.pallas_call(pair_kernel, in_specs=[any_spec, pl.BlockSpec(memory_space...  16.8 us
    dot_general x1, matrix products, project_inputs(): jnp.dot(hidden, w_dq, preferred_element_type=jnp.float32)  10.4 us
  transfers between devices with their start and end apart: 1, of which 0 were waited for; matrix products, arithmetic and copies ran while one was open for 0% of the time, Pallas kernels for 24%

commit v1 on v0

--- a/solution.py
+++ b/solution.py
@@ -40,7 +40,7 @@
     return jnp.concatenate([first_half * cos_t - second_half * sin_t, second_half * cos_t + first_half * sin_t], axis=-1)
 
 
-def query_kernel(cq, cos_t, sin_t, wq, wk, q_out, q_buf, k_buf, a_buf, r_buf):
+def query_kernel(cq, cos_t, sin_t, wq, wk, q_out, q_buf, q2_buf, k_buf, a_buf, r_buf):
     rows = cq.shape[0]
     heads, width, depth = wq.shape
     rank = wk.shape[0]
@@ -48,9 +48,12 @@
     half = (width - nope) // 2
     nt = (((1,), (1,)), ((), ()))
     k_buf[...] = wk[...].astype(jnp.float32).reshape(rank * heads, nope)
-    q_buf[...] = lax.dot_general(wq[...].reshape(heads * width, depth), cq[...], nt, preferred_element_type=jnp.float32)
+    part = heads // 2
+    for a, buf in enumerate((q_buf, q2_buf)):
+        buf[...] = lax.dot_general(wq[a * part:(a + 1) * part].reshape(part * width, depth), cq[...], nt, preferred_element_type=jnp.float32)
     for h in range(heads):
-        q = q_buf[h * width:(h + 1) * width, :].astype(jnp.bfloat16)
+        buf = (q_buf, q2_buf)[h // part]
+        q = buf[(h % part) * width:(h % part + 1) * width, :].astype(jnp.bfloat16)
         r1 = q[nope:nope + half].astype(jnp.float32)
         r2 = q[nope + half:].astype(jnp.float32)
         r = jnp.concatenate([r1 * cos_t[...] - r2 * sin_t[...], r2 * cos_t[...] + r1 * sin_t[...],
@@ -85,7 +88,8 @@
         out_specs=pl.BlockSpec((rows, hb, rank + 128), lambda i: (0, i, 0)),
         out_shape=jax.ShapeDtypeStruct((rows, heads, rank + 128), jnp.bfloat16),
         scratch_shapes=[
-            pltpu.VMEM((hb * width, rows), jnp.float32),
+            pltpu.VMEM((hb * width // 2, rows), jnp.float32),
+            pltpu.VMEM((hb * width // 2, rows), jnp.float32),
             pltpu.VMEM((rank * hb, nope), jnp.float32),
             pltpu.VMEM((rank // 128, rows * hb, 128), jnp.float32),
             pltpu.VMEM((rows * hb, 128), jnp.float32),
@@ -397,15 +401,15 @@
         slot = lax.rem(k, 2)
 
         def scale(t, _):
-            a = t // (rows // rb)
-            r0 = pl.multiple_of(lax.rem(t, rows // rb) * rb, rb)
-            h = k * CH + a
-            fo = column(f_buf, 0, r0, rb, h)
-            fm = column(f_buf, 1, r0, rb, h)
-            d_buf[h, pl.ds(r0, rb), :] = fo * own_buf[slot, a, pl.ds(r0, rb), :] + fm * d_buf[h, pl.ds(r0, rb), :]
+            r0 = pl.multiple_of(t * rb, rb)
+            for a in range(CH):
+                h = k * CH + a
+                fo = column(f_buf, 0, r0, rb, h)
+                fm = column(f_buf, 1, r0, rb, h)
+                d_buf[h, pl.ds(r0, rb), :] = fo * own_buf[slot, a, pl.ds(r0, rb), :] + fm * d_buf[h, pl.ds(r0, rb), :]
             return 0
 
-        lax.fori_loop(0, CH * (rows // rb), scale, 0)
+        lax.fori_loop(0, rows // rb, scale, 0)
         for c in outs(k):
             c.start()
 
@@ -445,7 +449,7 @@
             pltpu.VMEM((2, ml.shape[1] * 128, hh), jnp.float32),
             dma((n_chunk,)), dma((n_chunk,)), dma((n_sp,)), dma((n_sp,)), dma((2,)), dma((2, n_chunk)),
         ],
-        compiler_params=pltpu.CompilerParams(collective_id=cid, has_side_effects=True, vmem_limit_bytes=48 * 1024 * 1024),
+        compiler_params=pltpu.CompilerParams(collective_id=cid, has_side_effects=True, vmem_limit_bytes=VMEM_LIMIT),
         cost_estimate=pl.CostEstimate(flops=2_000_000_000, bytes_accessed=20_000_000, transcendentals=0),
         name=f"pair{rows}",
     )(u, ml)
@@ -531,34 +535,26 @@
         if n_rest:
             d_copy(k).wait_recv()
 
-            def scale(t, _):
-                a = t // (n_rest // rb)
-                r0 = pl.multiple_of(lax.rem(t, n_rest // rb) * rb, rb)
-                h = k * CH + a
-                fo = column(f_buf, 0, r0, rb, h)
-                fm = column(f_buf, 1, r0, rb, h)
-                d_buf[h, pl.ds(r0, rb), :] = fo * own_buf[slot, a, pl.ds(r0, rb), :] + fm * d_buf[h, pl.ds(r0, rb), :]
-                return 0
-
-            lax.fori_loop(0, CH * (n_rest // rb), scale, 0)
-
         @pl.when(lax.rem(k, wh // CH) == 0)
         def _():
             wuv_load(k // (wh // CH)).wait()
             k_buf[...] = wuv_buf[k // (wh // CH)].astype(jnp.float32).reshape(k_buf.shape)
 
-        def project(a, _):
+        for a in range(CH):
             h = k * CH + a
             wuv_h = k_buf[pl.ds(lax.rem(h, wh), rank, stride=wh), :].astype(jnp.bfloat16)
             u = keep_buf[slot, a] + got_buf[slot, a]
             if n_rest:
-                u = jnp.concatenate([u, d_buf[h]], axis=0)
+                parts = [u]
+                for r0 in range(0, n_rest, rb):
+                    fo = column(f_buf, 0, r0, rb, h)
+                    fm = column(f_buf, 1, r0, rb, h)
+                    parts.append(fo * own_buf[slot, a, pl.ds(r0, rb), :] + fm * d_buf[h, pl.ds(r0, rb), :])
+                u = jnp.concatenate(parts, axis=0)
             o = jnp.dot(u.astype(jnp.bfloat16), wuv_h, preferred_element_type=jnp.float32).astype(jnp.bfloat16)
             o_all[:, pl.ds(pl.multiple_of((core * hh + h) * vdim, 128), vdim)] = o
             o_out[h] = o.astype(jnp.float32)
-            return 0
-
-        lax.fori_loop(0, CH, project, 0)
+
         o_copy(k).start()
 
         @pl.when(k + 2 < n_chunk)
@@ -572,12 +568,9 @@
     def place_chunk(k, _):
         o_copy(k).wait_recv()
 
-        def place(a, _):
+        for a in range(CH):
             h = k * CH + a
             o_all[:, pl.ds(pl.multiple_of(((1 - core) * hh + h) * vdim, 128), vdim)] = o_in[h].astype(jnp.bfloat16)
-            return 0
-
-        lax.fori_loop(0, CH, place, 0)
         return 0
 
     lax.fori_loop(0, n_chunk, place_chunk, 0)

time: 320 us -> 316 us (0.988)
  waiting for transfers between devices: 0.01 us -> 9.03 us
  Pallas kernels: 283 us -> 274 us
    ppermute x1, waiting for transfers between devices: 0.01 us -> 9.03 us  [run(): got = lax.ppermute(give, 'sp', swap)]
    pallas_call x1, Pallas kernels: 107 us -> 99.5 us  [combine(): pl.pallas_call(functools.partial(combine_kernel, n_rest), in_specs=[any_s...]
  transfers between devices with their start and end apart: 1 -> 1, of which waited for: 0 -> 1; matrix products, arithmetic and copies ran while one was open for 0% -> 0% of each run, Pallas kernels for 24% -> 22%
where the time goes in v1:
time: 316 us; the launch traced here: 317 us
  Pallas kernels  274 us (87%)
  matrix products  19.3 us (6%)
  waiting for transfers between devices  9.03 us (3%)
  local copies, waits for them, and re-layouts  6.4 us (2%)
  other arithmetic  6.01 us (2%)
    pallas_call x2, Pallas kernels, attend(): pl.pallas_call(functools.partial(attend_kernel, score_scale, n_groups, fi...  127 us
    pallas_call x1, Pallas kernels, combine(): pl.pallas_call(functools.partial(combine_kernel, n_rest), in_specs=[any_s...  99.5 us
    pallas_call x1, Pallas kernels, queries(): pl.pallas_call(query_kernel, grid=(heads // hb,), in_specs=[pl.BlockSpec(...  31 us
    pallas_call x1, Pallas kernels, pair_reduce(): pl.pallas_call(pair_kernel, in_specs=[any_spec, pl.BlockSpec(memory_space...  16.2 us
    dot_general x1, matrix products, project_inputs(): jnp.dot(hidden, w_dq, preferred_element_type=jnp.float32)  10.4 us
    ppermute x1, waiting for transfers between devices, run(): got = lax.ppermute(give, 'sp', swap)  9.03 us
  transfers between devices with their start and end apart: 1, of which 1 were waited for; matrix products, arithmetic and copies ran while one was open for 0% of the time, Pallas kernels for 22%

profile of v1, /device:TPU:0, one launch (start us, length us, event | category | flops | bytes accessed | tf_op | source)
XLA Modules:
  0.0 317.0 jit_solution(9972278853903560966)
XLA Ops:
  0.6 1.3 fusion.16
  3.3 0.9 convert_reduce_fusion
  4.1 0.7 convert_element_type.75
  4.8 0.8 select_reduce_fusion
  5.7 0.7 convert_element_type.69
  6.4 0.2 multiply_sine_fusion.1
  6.6 0.8 fusion.4
  7.3 3.3 %convolution_convert_fusion = bf16[256,7168]{1,0:T(8,128)(2,1)S(1)} fusion(bf16[256,7168]{1,0:T(8,128)(2,1)} %param.15, s32[256]{0:T(256)S(1)} %convert_reduce_fusion), kind=kOutput, calls=%fused_computation | convolution fusion | flops 941424640 | bytes 7341056 | tf_op jit(solution)/shard_map/dot_general | solution.py:774
  10.6 5.7 %convolution_convert_fusion.2 = bf16[256,576]{0,1:T(8,128)(2,1)S(1)} fusion(bf16[256,7168]{1,0:T(8,128)(2,1)S(1)} %convolution_convert_fusion, bf16[7168,576]{0,1:T(8,128)(2,1)} %param.21), kind=kOutput, calls=%fused_computation.5 | convolution fusion | flops 2114076672 | bytes 12222464 | tf_op jit(solution)/shard_map/dot_general | solution.py:110
  16.3 10.4 %multiply_reduce_fusion = (f32[256]{0:T(256)S(1)}, f32[256,1536]{1,0:T(8,128)S(1)}) fusion(bf16[256,7168]{1,0:T(8,128)(2,1)S(1)} %convolution_convert_fusion, bf16[7168,1536]{1,0:T(8,128)(2,1)} %param.19), kind=kOutput, calls=%fused_computation.4 | convolution fusion | flops 5638717440 | bytes 27264000 | tf_op jit(solution)/shard_map/dot_general | solution.py:107
  26.7 0.2 multiply_convert_fusion.cq
  26.9 0.1 fusion.1
  27.0 0.1 fusion.3
  27.1 0.2 fusion.13
  27.3 31.0 %queries.1 = bf16[256,64,640]{2,1,0:T(8,128)(2,1)} custom-call(bf16[256,1536]{1,0:T(8,128)(2,1)S(1)} %multiply_convert_fusion.cq, f32[32,256]{1,0:T(8,128)S(1)} %get-tuple-element.184.cos_t, f32[32,256]{1,0:T(8,128)S(1)} %get-tuple-element.183.sin_t, bf16[64,192,1536]{2,1,0:T(8,128)(2,1)} %bitcast.12, bf16[512,64,128]{2,1,0:T(8,128)(2,1)} %wk.1), custom_call_target="tpu_custom_call" | custom-call | flops 11811160064 | bytes 70000000 | tf_op jit(solution)/shard_map/queries/pallas_call | solution.py:78
  58.4 254.6 %conditional.1 = (bf16[256,7168]{1,0:T(8,128)(2,1)}, bf16[256,512,512]{2,1,0:T(8,128)(2,1)}, bf16[256,64,512]{2,1,0:T(8,128)(2,1)}) conditional(s32[]{:T(128)} %clamp.3, (s32[256]{0:T(256)S(1)}, s32[256]{0:T(256)S(1)}, s32[1]{0:T(128)}, bf16[256,64,640]{2,1,0:T(8,128)(2,1)}, bf16[256,512]{0,1:T(8,128)(2,1)S(1)}, ...), branch_computations={%region_6.7_spmd, %region_7.8_spmd, %region_8.9_spmd} | conditional | flops 148028882944 | bytes 392048032 | solution.py:797
  58.4 0.1 copy.25.rope_new
  58.5 0.1 copy.24.lat_new
  58.6 56.2 %attend0_112.1 = (bf16[256,512,512]{2,1,0:T(8,128)(2,1)}, bf16[256,64,512]{2,1,0:T(8,128)(2,1)}, f32[64,112,512]{2,1,0:T(8,128)}, f32[2,1,64,128]{3,2,1,0:T(8,128)S(1)}) custom-call(s32[256]{0:T(256)S(1)} %get-tuple-element.94.perm, s32[256]{0:T(256)S(1)} %get-tuple-element.95.pos, s32[1]{0:T(128)} %get-tuple-element.96.base, ...), custom_call_target="tpu_custom_call" | custom-call | flops 63887638528 | bytes 146800640 | tf_op jit(solution)/shard_map/cond/branch_1_fun/attend0_112/pallas_call | solution.py:279
  114.9 0.0 copy-start.4
  114.9 0.6 copy-done.4
  115.5 16.2 %pair112.1 = (f32[32,56,512]{2,1,0:T(8,128)}, f32[32,56,512]{2,1,0:T(8,128)}) custom-call(f32[64,112,512]{2,1,0:T(8,128)} %get-tuple-element.102.u_ref, f32[2,1,64,128]{3,2,1,0:T(8,128)} %copy-done.4), custom_call_target="tpu_custom_call" | custom-call | flops 2000000000 | bytes 20000000 | tf_op jit(solution)/shard_map/cond/branch_1_fun/pair112/pallas_call | solution.py:440
  131.8 0.7 collective-permute-start.1
  132.4 0.0 copy-start.6
  132.5 70.5 %attend112_144.1 = (bf16[256,512,512]{2,1,0:T(8,128)(2,1)}, bf16[256,64,512]{2,1,0:T(8,128)(2,1)}, f32[64,144,512]{2,1,0:T(8,128)}, f32[2,2,64,128]{3,2,1,0:T(8,128)S(1)}) custom-call(s32[256]{0:T(256)S(1)} %get-tuple-element.94.perm, s32[256]{0:T(256)S(1)} %get-tuple-element.95.pos, ...), custom_call_target="tpu_custom_call", output_to_operand_aliasing={{0}: (8, {}), {1}: (9, {})} | custom-call | flops 82141249536 | bytes 188743680 | tf_op jit(solution)/shard_map/cond/branch_1_fun/attend112_144/pallas_call | solution.py:279
  203.0 0.0 copy-start.2
  203.0 0.6 copy-done.2
  203.6 0.0 copy-done.6
  203.6 0.8 copy.20.sel_ref
  204.4 9.0 %collective-permute-done.1.got_ref = f32[32,56,512]{2,1,0:T(8,128)} collective-permute-done((f32[32,56,512]{2,1,0:T(8,128)}, f32[32,56,512]{2,1,0:T(8,128)}, u32[]{:S(2)}, u32[]{:S(2)}) %collective-permute-start.1) | collective-permute-done | bytes 3670048 | tf_op jit(solution)/shard_map/cond/branch_1_fun/ppermute | solution.py:789
  213.4 99.5 %combine112.1 = bf16[256,7168]{1,0:T(8,128)(2,1)} custom-call(f32[32,56,512]{2,1,0:T(8,128)} %get-tuple-element.104.keep_ref, f32[32,56,512]{2,1,0:T(8,128)} %collective-permute-done.1.got_ref, bf16[512,64,128]{2,1,0:T(8,128)(2,1)} %get-tuple-element.106.wuv_ref, bf16[8192,7168]{1,0:T(8,128)(2,1)} %get-tuple-element.107.wout_ref, ...), custom_call_target="tpu_custom_call" | custom-call | tf_op jit(solution)/shard_map/cond/branch_1_fun/combine112/pallas_call | solution.py:741
  312.9 4.1 %copy.42 = bf16[256,7168]{1,0:T(8,128)(2,1)} copy(bf16[256,7168]{1,0:T(8,128)(2,1)} %get-tuple-element.199) | data formatting | bytes 7340032
  (6 shorter events, 0.0 us)
Async XLA Ops:
  114.9 0.6 copy-start.4
  131.8 81.7 %collective-permute-start.1 = (f32[32,56,512]{2,1,0:T(8,128)}, f32[32,56,512]{2,1,0:T(8,128)}, u32[]{:S(2)}, u32[]{:S(2)}) collective-permute-start(f32[32,56,512]{2,1,0:T(8,128)} %get-tuple-element.105), channel_id=1, source_target_pairs={{0,2},{1,3},{2,0},{3,1},{4,6},{5,7},{6,4},{7,5}} | collective-permute-start | bytes 11010056 | tf_op jit(solution)/shard_map/cond/branch_1_fun/ppermute | solution.py:789
  132.4 71.2 %copy-start.6 = (bf16[256,256]{0,1:T(8,128)(2,1)S(1)}, bf16[256,256]{0,1:T(8,128)(2,1)}, u32[]{:S(2)}) copy-start(bf16[256,256]{0,1:T(8,128)(2,1)} %get-tuple-element.109) | copy-start | bytes 393220 | tf_op jit(solution)/shard_map/cond
  203.0 0.7 copy-start.2
